TPU v7x, 32 devices: a whole 2x2x4 slice. The times are simulated.
32 devices in a mesh: blk: 8 (over y, x, core), width: 4 (over z).
Axes of the slice: x: 2, y: 2, z: 4, core: 2. Of those that a mesh axis runs over, the one named last changes fastest.
Arguments:
- inputs: bfloat16 [8, 128, 2048], P('blk', None, 'width'), may hold values from -6 to 6
- encoder: bfloat16 [8, 2048, 4096], P('blk', 'width'), may hold values from -0.125 to 0.125
- enc_bias: float32 [8, 4096], P('blk'), may hold values from -3 to 3
- active_blocks: int32 [8, 128, 32], P('blk'), may hold values 0 or 1
- near_decoders: bfloat16 [8, 4, 4096, 2048], P('blk', None, None, 'width'), may hold values from -0.09375 to 0.09375
- far_decoders: bfloat16 [8, 2048, 2048], P('blk', None, 'width'), may hold values from -0.09375 to 0.09375
- targets: bfloat16 [8, 128, 2048], P('blk', None, 'width'), may hold values from -6 to 6
Outputs:
- reconstruction: float32 [8, 128, 2048], P('blk', None, 'width')
- grad_encoder: bfloat16 [8, 2048, 4096], P('blk', 'width')
- grad_bias: float32 [8, 4096], P('blk')
All inputs are finite; a program needn't handle non-finite values. No bound on the sum of `active_blocks` on one device may be relied on, other than what follows from the above.
Results may differ from a plain program's by a relative error of at most 0.011.
Values may be sent and summed in bfloat16 or wider, within the bound.
A program may use at most 128 MiB of HBM per device.

v0:
```python
import jax
import jax.numpy as jnp
from jax import lax
from jax.sharding import PartitionSpec as P

FBLK = 128


def shifted(block, axis, distance):
    devices = range(lax.axis_size(axis))
    route = [(i - distance, i) for i in devices if i - distance in devices]
    return lax.ppermute(block, axis, route)


def expand_mask(blocks):
    token_count, block_count = blocks.shape
    spread = jnp.broadcast_to(
        blocks.astype(jnp.float32)[:, :, None], (token_count, block_count, FBLK)
    )
    return spread.reshape(token_count, block_count * FBLK)


def forward_product(activations, weights):
    return jnp.dot(activations, weights, preferred_element_type=jnp.float32)


def backward_product(grads, weights):
    return lax.dot_general(
        grads, weights, (((1,), (1,)), ((), ())), preferred_element_type=jnp.float32
    )


def pick_row(stacked, position):
    return lax.dynamic_index_in_dim(stacked, position, 0, keepdims=False)


def on_device(inputs, encoder, enc_bias, active_blocks, near_decoders, far_decoders, targets):
    layers = lax.axis_size("blk")
    cycle_index = lax.axis_index("blk")
    near_count = layers // 2
    half_rows = far_decoders.shape[1]
    local_in = inputs[0]
    tok_rows = local_in.shape[0]
    width_cols = targets.shape[2]
    mask_full = expand_mask(active_blocks[0])
    partial_pre = jnp.dot(local_in, encoder[0], preferred_element_type=jnp.float32)
    shard_pre = lax.psum_scatter(partial_pre, "width", scatter_dimension=1, tiled=True)
    columns = shard_pre.shape[1]
    start_col = lax.axis_index("width") * columns
    mask_part = lax.dynamic_slice_in_dim(mask_full, start_col, columns, 1)
    bias_part = lax.dynamic_slice_in_dim(enc_bias[0], start_col, columns, 0)
    act_part = (mask_part * (shard_pre + bias_part)).astype(jnp.bfloat16)
    activations = lax.all_gather(act_part, "width", axis=1, tiled=True)
    buffer = jnp.zeros((layers, tok_rows, width_cols), jnp.float32)
    buffer = buffer.at[cycle_index].add(forward_product(activations, near_decoders[0, 0]))
    for offset in range(1, near_count):
        inside = cycle_index >= offset
        wrap_row = (cycle_index - offset + layers) % layers
        slot = near_decoders[0, offset]
        remote = shifted(activations, "blk", offset)
        source = jnp.where(inside, remote, activations)
        target_row = jnp.where(inside, cycle_index, wrap_row)
        buffer = buffer.at[target_row].add(forward_product(source, slot))
    arrived_high = shifted(activations[:, half_rows:], "blk", near_count)
    upper_half = cycle_index >= near_count
    far_source = jnp.where(upper_half, arrived_high, activations[:, :half_rows])
    far_target = cycle_index % near_count + near_count
    buffer = buffer.at[far_target].add(forward_product(far_source, far_decoders[0]))
    reconstruction = lax.psum_scatter(buffer, "blk", scatter_dimension=0, tiled=True)
    out_grad = (reconstruction - targets.astype(jnp.float32)).astype(jnp.bfloat16)
    all_grads = lax.all_gather(out_grad, "blk", axis=0, tiled=True)
    own_grad = backward_product(pick_row(all_grads, cycle_index), near_decoders[0, 0])
    for offset in range(1, near_count):
        inside = cycle_index >= offset
        wrap_row = (cycle_index - offset + layers) % layers
        slot = near_decoders[0, offset]
        target_row = jnp.where(inside, cycle_index, wrap_row)
        term = backward_product(pick_row(all_grads, target_row), slot)
        own_grad = own_grad + jnp.where(inside, 0.0, term)
        outgoing = jnp.where(inside, term, 0.0)
        own_grad = own_grad + shifted(outgoing, "blk", -offset)
    far_grad = backward_product(pick_row(all_grads, far_target), far_decoders[0])
    returned = shifted(jnp.where(upper_half, far_grad, 0.0), "blk", -near_count)
    lower_add = jnp.where(upper_half, 0.0, far_grad)
    own_grad = own_grad + jnp.concatenate([lower_add, returned], axis=1)
    grad_part = lax.psum_scatter(own_grad, "width", scatter_dimension=1, tiled=True)
    columns = grad_part.shape[1]
    start_col = lax.axis_index("width") * columns
    mask_slice = lax.dynamic_slice_in_dim(mask_full, start_col, columns, 1)
    pre_grad = lax.all_gather(
        (mask_slice * grad_part).astype(jnp.bfloat16), "width", axis=1, tiled=True
    )
    enc_grad = lax.dot_general(
        local_in, pre_grad, (((0,), (0,)), ((), ())), preferred_element_type=jnp.float32
    )
    bias_grad = jnp.sum(pre_grad.astype(jnp.float32), axis=0)
    return (reconstruction, enc_grad.astype(jnp.bfloat16)[None], bias_grad[None])


def solution(mesh):
    return jax.shard_map(
        on_device,
        mesh=mesh,
        in_specs=(
            P("blk", None, "width"),
            P("blk", "width", None),
            P("blk", None),
            P("blk", None, None),
            P("blk", None, None, "width"),
            P("blk", None, "width"),
            P("blk", None, "width"),
        ),
        out_specs=(P("blk", None, "width"), P("blk", "width", None), P("blk", None)),
        check_vma=False,
    )
```

profile of v0, /device:TPU:16, one launch (start us, length us, event | category | flops | bytes accessed | tf_op | source)
XLA Modules:
  0.0 471.8 jit_solution(9769207703917947747)
XLA Ops:
  7.2 4.4 fusion.22
  11.7 0.0 all-gather.4.cloned.1.call-start
  11.7 0.6 copy-done.7
  12.4 0.1 copy.12
  12.5 0.6 broadcast_in_dim.38
  13.1 3.0 copy.16
  16.1 0.7 constant_dynamic-slice_fusion
  16.7 39.0 %reduce-scatter.4.cloned.1.call-done = f32[128,1024]{1,0:T(8,128)} async-done(((f32[128,4096]{1,0:T(8,128)}), f32[128,1024]{1,0:T(8,128)}) %reduce-scatter.4.cloned.1.call-update) | async-done | bytes 524304 | tf_op jit(solution)/shard_map/reduce_scatter | solution.py:47
  55.8 2.0 multiply_convert_fusion.1
  57.8 27.5 %all-gather.4.cloned.1.call-done = bf16[128,4096]{1,0:T(8,128)(2,1)} async-done(((bf16[128,1024]{1,0:T(8,128)(2,1)}), bf16[128,4096]{1,0:T(8,128)(2,1)}) %all-gather.4.cloned.1.call-update) | async-done | bytes 1048592 | tf_op jit(solution)/shard_map/all_gather | solution.py:53
  85.3 2.4 collective-permute-start
  87.7 4.1 collective-permute-start.1
  91.7 0.7 and_reduce_fusion.4
  92.4 0.8 and_reduce_fusion
  93.3 1.1 slice.123
  94.4 2.4 collective-permute-start.3
  96.8 2.2 collective-permute-start.2
  99.1 1.6 broadcast_in_dim.37
  100.6 5.3 %fusion.90 = f32[8,128,512]{2,1,0:T(8,128)} fusion(f32[8,128,512]{2,1,0:T(8,128)} %broadcast_in_dim.37, s32[]{:T(128)} %select_n.141, bf16[128,4096]{1,0:T(8,128)(2,1)S(1)} %copy-done.3, bf16[1,4,4096,512]{3,2,1,0:T(8,128)(2,1)} %param.21, pred[]{:T(512)} %and_reduce_fusion.4), kind=kOutput, calls=%fused_computation.58 | convolution fusion | flops 536936448 | bytes 5506048 | tf_op jit(solution)/shard_map/dot_general | solution.py:24
  105.9 4.2 fusion.72
  110.1 4.4 collective-permute-done.1
  114.6 3.1 fusion.63
  117.7 16.9 %collective-permute-done.2 = bf16[128,4096]{1,0:T(8,128)(2,1)S(1)} collective-permute-done((bf16[128,4096]{1,0:T(8,128)(2,1)}, bf16[128,4096]{1,0:T(8,128)(2,1)S(1)}, u32[]{:S(2)}, u32[]{:S(2)}) %collective-permute-start.2) | collective-permute-done | bytes 1048608 | tf_op jit(solution)/shard_map/ppermute | solution.py:12
  134.5 3.0 fusion.54
  137.5 9.1 %collective-permute-done.3 = bf16[128,2048]{1,0:T(8,128)(2,1)S(1)} collective-permute-done((bf16[128,2048]{1,0:T(8,128)(2,1)S(1)}, bf16[128,2048]{1,0:T(8,128)(2,1)S(1)}, u32[]{:S(2)}, u32[]{:S(2)}) %collective-permute-start.3) | collective-permute-done | bytes 524320 | tf_op jit(solution)/shard_map/ppermute | solution.py:12
  146.6 2.8 fusion.81
  149.4 0.0 all-gather.6.cloned.1.call-start
  149.5 55.5 %reduce-scatter.6.cloned.1.call-done = f32[1,128,512]{2,1,0:T(8,128)} async-done(((f32[8,128,512]{2,1,0:T(8,128)}), f32[1,128,512]{2,1,0:T(8,128)}) %reduce-scatter.6.cloned.1.call-update) | async-done | bytes 262160 | tf_op jit(solution)/shard_map/reduce_scatter | solution.py:69
  205.0 1.6 subtract_convert_fusion
  206.7 24.0 %all-gather.6.cloned.1.call-done = bf16[8,128,512]{2,1,0:T(8,128)(2,1)} async-done(((bf16[1,128,512]{2,1,0:T(8,128)(2,1)}), bf16[8,128,512]{2,1,0:T(8,128)(2,1)}) %all-gather.6.cloned.1.call-update) | async-done | bytes 1048592 | tf_op jit(solution)/shard_map/all_gather | solution.py:71
  230.7 3.8 broadcast_select_fusion.2
  234.5 1.3 collective-permute-start.4
  235.8 3.7 broadcast_select_fusion
  239.5 1.3 collective-permute-start.5
  240.8 3.7 broadcast_select_fusion.1
  244.5 1.3 collective-permute-start.6
  245.8 0.8 broadcast_select_fusion.4
  246.6 1.5 collective-permute-start.7
  248.1 49.3 %collective-permute-done.7 = f32[128,2048]{1,0:T(8,128)S(1)} collective-permute-done((f32[128,2048]{1,0:T(8,128)S(1)}, f32[128,2048]{1,0:T(8,128)S(1)}, u32[]{:S(2)}, u32[]{:S(2)}) %collective-permute-start.7) | collective-permute-done | bytes 1048608 | tf_op jit(solution)/shard_map/ppermute | solution.py:12
  297.4 26.9 %collective-permute-done.5 = f32[128,4096]{1,0:T(8,128)S(1)} collective-permute-done((f32[128,4096]{1,0:T(8,128)S(1)}, f32[128,4096]{1,0:T(8,128)S(1)}, u32[]{:S(2)}, u32[]{:S(2)}) %collective-permute-start.5) | collective-permute-done | bytes 2097184 | tf_op jit(solution)/shard_map/ppermute | solution.py:12
  324.3 5.3 %collective-permute-done.6 = f32[128,4096]{1,0:T(8,128)S(1)} collective-permute-done((f32[128,4096]{1,0:T(8,128)S(1)}, f32[128,4096]{1,0:T(8,128)S(1)}, u32[]{:S(2)}, u32[]{:S(2)}) %collective-permute-start.6) | collective-permute-done | bytes 2097184 | tf_op jit(solution)/shard_map/ppermute | solution.py:12
  329.7 5.2 %fusion.6 = f32[128,4096]{1,0:T(8,128)} fusion(f32[128,4096]{1,0:T(8,128)S(1)} %collective-permute-done.6, f32[128,4096]{1,0:T(8,128)S(1)} %collective-permute-done.5, f32[128,4096]{1,0:T(8,128)S(1)} %collective-permute-done.4, bf16[1,4,4096,512]{3,2,1,0:T(8,128)(2,1)} %param.21, f32[128,2048]{1,0:T(8,128)S(1)} %collective-permute-done.7, ...), kind=kOutput, calls=%fused_computation.8 | convolution fusion | flops 542638080 | bytes 21103108 | tf_op jit(solution)/shard_map/dot_general | solution.py:28
  335.0 88.8 %reduce-scatter.8.cloned.1.call-done = f32[128,1024]{1,0:T(8,128)} async-done(((f32[128,4096]{1,0:T(8,128)}), f32[128,1024]{1,0:T(8,128)}) %reduce-scatter.8.cloned.1.call-update) | async-done | bytes 524304 | tf_op jit(solution)/shard_map/reduce_scatter | solution.py:86
  423.8 2.0 multiply_convert_fusion
  425.8 27.5 %all-gather.8.cloned.1.call-done = bf16[128,4096]{1,0:T(8,128)(2,1)} async-done(((bf16[128,1024]{1,0:T(8,128)(2,1)}), bf16[128,4096]{1,0:T(8,128)(2,1)}) %all-gather.8.cloned.1.call-update) | async-done | bytes 1048592 | tf_op jit(solution)/shard_map/all_gather | solution.py:90
  453.3 4.4 fusion
  457.8 6.4 %copy.13 = bf16[1,512,4096]{2,1,0:T(8,128)(2,1)} copy(bf16[1,512,4096]{1,2,0:T(8,128)(2,1)} %fusion) | data formatting | bytes 8388608
  464.2 0.8 convert_reduce_fusion
  (30 shorter events, 0.3 us)
Async XLA Ops:
  7.2 139.5 %copy-start = (bf16[1,2048,512]{2,1,0:T(8,128)(2,1)S(1)}, bf16[1,2048,512]{2,1,0:T(8,128)(2,1)}, u32[]{:S(2)}) copy-start(bf16[1,2048,512]{2,1,0:T(8,128)(2,1)} %param.22) | copy-start | bytes 6291460
  7.2 48.6 %reduce-scatter.4.cloned.1.call-start = ((), (), s32[]{:S(2)}) async-start(), calls=%async_computation.3 | async-start | bytes 2621440 | tf_op jit(solution)/shard_map/reduce_scatter | solution.py:47
  11.7 0.7 copy-start.7
  11.7 73.6 %all-gather.4.cloned.1.call-start = ((), (), s32[]{:S(2)}) async-start(), calls=%async_computation.4 | async-start | bytes 1310720 | tf_op jit(solution)/shard_map/all_gather | solution.py:53
  13.1 78.7 %copy-start.8 = (s32[3]{0:T(128)S(1)}, s32[3]{0:T(128)}, u32[]{:S(2)}) copy-start(s32[3]{0:T(128)} %constant.171.clone.1) | copy-start | bytes 40
  57.8 147.2 %reduce-scatter.6.cloned.1.call-start = ((), (), s32[]{:S(2)}) async-start(), calls=%async_computation.5 | async-start | bytes 2359296 | tf_op jit(solution)/shard_map/reduce_scatter | solution.py:69
  85.3 15.3 %copy-start.3 = (bf16[128,4096]{1,0:T(8,128)(2,1)S(1)}, bf16[128,4096]{1,0:T(8,128)(2,1)}, u32[]{:S(2)}) copy-start(bf16[128,4096]{1,0:T(8,128)(2,1)} %all-gather.4.cloned.1.call-done) | copy-start | bytes 3145732
  85.3 20.6 %collective-permute-start = (bf16[128,4096]{1,0:T(8,128)(2,1)}, bf16[128,4096]{1,0:T(8,128)(2,1)}, u32[]{:S(2)}, u32[]{:S(2)}) collective-permute-start(bf16[128,4096]{1,0:T(8,128)(2,1)} %all-gather.4.cloned.1.call-done), channel_id=1, source_target_pairs={{0,4},{4,8},{8,12},{12,16},{16,20},{20,24},{24,28},{1,5},{5,9},{9,... | collective-permute-start | bytes 3145736 | tf_op jit(solution)/shard_map/ppermute | solution.py:12
  87.7 26.9 %collective-permute-start.1 = (bf16[128,4096]{1,0:T(8,128)(2,1)}, bf16[128,4096]{1,0:T(8,128)(2,1)}, u32[]{:S(2)}, u32[]{:S(2)}) collective-permute-start(bf16[128,4096]{1,0:T(8,128)(2,1)} %all-gather.4.cloned.1.call-done), channel_id=1, source_target_pairs={{0,8},{4,12},{8,16},{12,20},{16,24},{20,28},{1,9},{5,13},{9,17},{1... | collective-permute-start | bytes 3145736 | tf_op jit(solution)/shard_map/ppermute | solution.py:12
  94.4 52.3 %collective-permute-start.3 = (bf16[128,2048]{1,0:T(8,128)(2,1)S(1)}, bf16[128,2048]{1,0:T(8,128)(2,1)S(1)}, u32[]{:S(2)}, u32[]{:S(2)}) collective-permute-start(bf16[128,2048]{1,0:T(8,128)(2,1)S(1)} %slice.123), channel_id=1, source_target_pairs={{0,16},{4,20},{8,24},{12,28},{1,17},{5,21},{9,25},{13,29},{2,18},{... | collective-permute-start | bytes 1572872 | tf_op jit(solution)/shard_map/ppermute | solution.py:12
  96.8 37.8 %collective-permute-start.2 = (bf16[128,4096]{1,0:T(8,128)(2,1)}, bf16[128,4096]{1,0:T(8,128)(2,1)S(1)}, u32[]{:S(2)}, u32[]{:S(2)}) collective-permute-start(bf16[128,4096]{1,0:T(8,128)(2,1)} %all-gather.4.cloned.1.call-done), channel_id=1, source_target_pairs={{0,12},{4,16},{8,20},{12,24},{16,28},{1,13},{5,17},{9,21},{13,25},... | collective-permute-start | bytes 3145736 | tf_op jit(solution)/shard_map/ppermute | solution.py:12
  99.0 15.5 %copy-start.1 = (bf16[1,4,4096,512]{3,2,1,0:T(8,128)(2,1)S(1)}, bf16[1,4,4096,512]{3,2,1,0:T(8,128)(2,1)}, u32[]{:S(2)}) copy-start(bf16[1,4,4096,512]{3,2,1,0:T(8,128)(2,1)} %param.21) | copy-start | bytes 50331652
  146.6 58.4 %copy-start.6 = (bf16[1,128,512]{2,1,0:T(8,128)(2,1)S(1)}, bf16[1,128,512]{2,1,0:T(8,128)(2,1)}, u32[]{:S(2)}) copy-start(bf16[1,128,512]{2,1,0:T(8,128)(2,1)} %param.23) | copy-start | bytes 393220
  149.4 81.3 %all-gather.6.cloned.1.call-start = ((), (), s32[]{:S(2)}) async-start(), calls=%async_computation.6 | async-start | bytes 1179648 | tf_op jit(solution)/shard_map/all_gather | solution.py:71
  206.6 217.2 %reduce-scatter.8.cloned.1.call-start = ((), (), s32[]{:S(2)}) async-start(), calls=%async_computation.7 | async-start | bytes 2621440 | tf_op jit(solution)/shard_map/reduce_scatter | solution.py:86
  230.7 5.1 %copy-start.5 = (bf16[8,128,512]{2,1,0:T(8,128)(2,1)S(1)}, bf16[8,128,512]{2,1,0:T(8,128)(2,1)}, u32[]{:S(2)}) copy-start(bf16[8,128,512]{2,1,0:T(8,128)(2,1)} %all-gather.6.cloned.1.call-done) | copy-start | bytes 3145732
  234.5 62.9 %collective-permute-start.4 = (f32[128,4096]{1,0:T(8,128)S(1)}, f32[128,4096]{1,0:T(8,128)S(1)}, u32[]{:S(2)}, u32[]{:S(2)}) collective-permute-start(f32[128,4096]{1,0:T(8,128)S(1)} %get-tuple-element.81), channel_id=1, source_target_pairs={{4,0},{8,4},{12,8},{16,12},{20,16},{24,20},{28,24},{5,1},{9,5},{13... | collective-permute-start | bytes 6291464 | tf_op jit(solution)/shard_map/ppermute | solution.py:12
  239.5 84.8 %collective-permute-start.5 = (f32[128,4096]{1,0:T(8,128)S(1)}, f32[128,4096]{1,0:T(8,128)S(1)}, u32[]{:S(2)}, u32[]{:S(2)}) collective-permute-start(f32[128,4096]{1,0:T(8,128)S(1)} %get-tuple-element.79), channel_id=1, source_target_pairs={{8,0},{12,4},{16,8},{20,12},{24,16},{28,20},{9,1},{13,5},{17,9},{2... | collective-permute-start | bytes 6291464 | tf_op jit(solution)/shard_map/ppermute | solution.py:12
  244.5 85.2 %collective-permute-start.6 = (f32[128,4096]{1,0:T(8,128)S(1)}, f32[128,4096]{1,0:T(8,128)S(1)}, u32[]{:S(2)}, u32[]{:S(2)}) collective-permute-start(f32[128,4096]{1,0:T(8,128)S(1)} %get-tuple-element.77), channel_id=1, source_target_pairs={{12,0},{16,4},{20,8},{24,12},{28,16},{13,1},{17,5},{21,9},{25,13},... | collective-permute-start | bytes 6291464 | tf_op jit(solution)/shard_map/ppermute | solution.py:12
  246.6 50.8 %collective-permute-start.7 = (f32[128,2048]{1,0:T(8,128)S(1)}, f32[128,2048]{1,0:T(8,128)S(1)}, u32[]{:S(2)}, u32[]{:S(2)}) collective-permute-start(f32[128,2048]{1,0:T(8,128)S(1)} %get-tuple-element.74), channel_id=1, source_target_pairs={{16,0},{20,4},{24,8},{28,12},{17,1},{21,5},{25,9},{29,13},{18,2},{... | collective-permute-start | bytes 3145736 | tf_op jit(solution)/shard_map/ppermute | solution.py:12
  334.9 118.4 %copy-start.4 = (bf16[1,128,512]{2,1,0:T(8,128)(2,1)S(1)}, bf16[1,128,512]{2,1,0:T(8,128)(2,1)}, u32[]{:S(2)}) copy-start(bf16[1,128,512]{2,1,0:T(8,128)(2,1)} %param.17) | copy-start | bytes 393220
  334.9 118.4 %all-gather.8.cloned.1.call-start = ((), (), s32[]{:S(2)}) async-start(), calls=%async_computation.8 | async-start | bytes 1310720 | tf_op jit(solution)/shard_map/all_gather | solution.py:90
  457.8 6.4 %copy-start.2 = (bf16[128,4096]{1,0:T(8,128)(2,1)S(1)}, bf16[128,4096]{1,0:T(8,128)(2,1)}, u32[]{:S(2)}) copy-start(bf16[128,4096]{1,0:T(8,128)(2,1)} %all-gather.8.cloned.1.call-done) | copy-start | bytes 3145732
Sparse Core Ops, SparseCore 0:
  11.8 43.9 reduce-scatter.3
  57.9 27.3 all-gather.3
  149.5 55.3 reduce-scatter.5
  207.3 23.3 all-gather.5
  335.1 88.7 reduce-scatter.7
  425.9 27.3 all-gather.7
where the time goes:
time: 475 us; the launch traced here: 472 us
  waiting for transfers between devices  374 us (79%)
  matrix products  44.4 us (9%)
  starting transfers between devices  16.7 us (4%)
  between operations  14.3 us (3%)
  local copies, waits for them, and re-layouts  14.1 us (3%)
  other arithmetic  7.88 us (2%)
    ppermute x8, waiting for transfers between devices, shifted(): return lax.ppermute(block, axis, route)  112 us
    reduce_scatter x1, waiting for transfers between devices, on_device(): lax.psum_scatter(own_grad, 'width', scatter_dimension=1, tiled=True)  88.8 us
    reduce_scatter x1, waiting for transfers between devices, on_device(): lax.psum_scatter(buffer, 'blk', scatter_dimension=0, tiled=True)  55.5 us
    reduce_scatter x1, waiting for transfers between devices, on_device(): lax.psum_scatter(partial_pre, 'width', scatter_dimension=1, tiled=True)  39 us
    all_gather x1, waiting for transfers between devices, on_device(): lax.all_gather((mask_slice * grad_part).astype(jnp.bfloat16), 'width', ax...  27.5 us
    all_gather x1, waiting for transfers between devices, on_device(): activations = lax.all_gather(act_part, 'width', axis=1, tiled=True)  27.5 us
    all_gather x1, waiting for transfers between devices, on_device(): all_grads = lax.all_gather(out_grad, 'blk', axis=0, tiled=True)  24 us
    dot_general x5, matrix products, forward_product(): return jnp.dot(activations, weights, preferred_element_type=jnp.float32)  18.3 us
  transfers between devices with their start and end apart: 14, of which 12 were waited for; matrix products, arithmetic and copies ran while one was open for 7% of the time, Pallas kernels for 0%

commit v1 on v0

v1 whole, which is shorter than its diff:
```python
import functools

import jax
import jax.numpy as jnp
from jax import lax
from jax.experimental import pallas as pl
from jax.experimental.pallas import tpu as pltpu
from jax.sharding import PartitionSpec as P

BF = jnp.bfloat16
F32 = jnp.float32


def dot(a, b):
    return jnp.dot(a, b, preferred_element_type=F32)


def dot_t(a, b):
    return lax.dot_general(a, b, (((1,), (1,)), ((), ())), preferred_element_type=F32)


def step_kernel(B, W, C, FBLK, x_ref, enc_hbm, bias_ref, blocks_ref, near_hbm, far_hbm, tgt_ref,
                recon_ref, pg_ref,
                enc, near, far, z1_out, z1_in, acts, p_out, p_in, og, terms, duo, ret, own, z3_out, z3_in, pg,
                enc_sem, near_sem, far_sem, z1_s, z1_r, z2_s, z2_r, ad_s, af_s, a_r, p_s, p_r, o_s, o_r,
                d_s, d_r, r_s, r_r, z3_s, z3_r, z4_s, z4_r):
    N = B // 2
    H = W // 2
    b = lax.axis_index("blk")
    w = lax.axis_index("width")
    even = lax.rem(b, 2) == 0
    odd = lax.rem(b, 2) == 1

    def col(j):
        return pl.ds(pl.multiple_of(j * C, C), C)

    def blk(d):
        return lax.rem(w + d, W)

    def remote(src, dst, s, r, to_b, to_w):
        return pltpu.make_async_remote_copy(src_ref=src, dst_ref=dst, send_sem=s, recv_sem=r,
                                            device_id=(to_b, to_w), device_id_type=pl.DeviceIdType.MESH)

    def loop(lo, hi, body):
        def run(i, carry):
            body(i)
            return carry
        lax.fori_loop(lo, hi, run, 0)

    def enc_copy(j):
        return pltpu.make_async_copy(enc_hbm.at[:, col(j)], enc.at[:, col(j)], enc_sem.at[j])

    def near_copy(k):
        return pltpu.make_async_copy(near_hbm.at[k], near.at[k], near_sem.at[k])

    far_copy = pltpu.make_async_copy(far_hbm, far, far_sem)

    def z1(j):
        return remote(z1_out.at[j], z1_in.at[w], z1_s.at[j], z1_r.at[w], b, j)

    def z1_arrival(j):
        return remote(z1_out.at[j], z1_in.at[j], z1_s.at[j], z1_r.at[j], b, j)

    def z2(j):
        return remote(acts.at[0, w], acts.at[0, w], z2_s.at[j], z2_r.at[w], b, j)

    def z2_arrival(j):
        return remote(acts.at[0, j], acts.at[0, j], z2_s.at[j], z2_r.at[j], b, j)

    def z3(j):
        return remote(z3_out.at[j], z3_in.at[w], z3_s.at[j], z3_r.at[w], b, j)

    def z3_arrival(j):
        return remote(z3_out.at[j], z3_in.at[j], z3_s.at[j], z3_r.at[j], b, j)

    def z4(j):
        return remote(pg.at[w], pg.at[w], z4_s.at[j], z4_r.at[w], b, j)

    def z4_arrival(j):
        return remote(pg.at[j], pg.at[j], z4_s.at[j], z4_r.at[j], b, j)

    def act_direct(k, j):
        return remote(acts.at[0, j], acts.at[k, j], ad_s.at[k, j], a_r.at[k, j], b + k, w)

    def act_pass(k_from, k, j, to):
        return remote(acts.at[k_from, j], acts.at[k, j], af_s.at[k, j], a_r.at[k, j], to, w)

    def share(k):
        return remote(p_out.at[k], p_in.at[k], p_s.at[k], p_r.at[k], b - k + B, w)

    def out_grad(k):
        return remote(og.at[0], og.at[k], o_s.at[k], o_r.at[k], b + k - B, w)

    def duo_copy(k_from, k, j, to):
        return remote(terms.at[k_from, j], duo.at[k, j], d_s.at[k_from, j], d_r.at[k, j], to, w)

    def ret_copy(k, j, to):
        return remote(terms.at[k, j], ret.at[k, j], r_s.at[k, j], r_r.at[k, j], to, w)

    loop(1, W + 1, lambda d: enc_copy(blk(d)).start())
    for k in range(N):
        near_copy(k).start()
    far_copy.start()

    barrier = pltpu.get_barrier_semaphore()
    for d in range(1, W):
        pl.semaphore_signal(barrier, inc=1, device_id=(b, lax.rem(w + d, W)), device_id_type=pl.DeviceIdType.MESH)
    for d in range(1, B):
        pl.semaphore_signal(barrier, inc=1, device_id=(lax.rem(b + d, B), w), device_id_type=pl.DeviceIdType.MESH)
    pl.semaphore_wait(barrier, W + B - 2)

    def first(d):
        j = blk(d)
        enc_copy(j).wait()
        z1_out[j] = dot(x_ref[...], enc[:, col(j)]).astype(BF)
        z1(j).start()

    loop(1, W, first)
    enc_copy(w).wait()
    own[w] = dot(x_ref[...], enc[:, col(w)]) + bias_ref[:, col(w)]
    fb = blocks_ref.shape[1]
    row_id = lax.broadcasted_iota(jnp.int32, (fb, C), 0) - w * (C // FBLK)
    lane_id = lax.broadcasted_iota(jnp.int32, (fb, C), 1) // FBLK
    spread = jnp.where(row_id == lane_id, 1.0, 0.0).astype(BF)

    def mask():
        return dot(blocks_ref[...].astype(F32).astype(BF), spread)

    def gather1(d):
        j = blk(d)
        z1_arrival(j).wait_recv()
        own[w] += z1_in[j].astype(F32)

    loop(1, W, gather1)
    acts[0, w] = (mask() * own[w]).astype(BF)
    loop(1, W, lambda d: z2(blk(d)).start())

    def act_sends(j, act):
        for k in range(2, N, 2):
            @pl.when(b + k < B)
            def _():
                act(act_direct(k, j))

        @pl.when(even)
        def _():
            act(act_pass(0, 1, j, b + 1))

        @pl.when(odd & (b + N - 1 < B))
        def _():
            act(act_direct(N - 1, j))

        @pl.when(even & (b + N < B) & (j >= H))
        def _():
            act(act_direct(N, j))

    start = lambda c: c.start()
    end = lambda c: c.wait_send()
    act_sends(w, start)

    def gather2(d):
        j = blk(d)
        z2_arrival(j).wait_recv()
        act_sends(j, start)

    loop(1, W, gather2)
    for k in range(N):
        near_copy(k).wait()
    far_copy.wait()

    def own_term(k):
        def body(j):
            recon_ref[...] += dot(acts[0, j], near[k, col(j), :])
        return body

    def far_term(j):
        recon_ref[...] += dot(acts[0, j], far[col(j), :])

    for k in range(1, N + 1):
        @pl.when(b < k)
        def _():
            recon_ref[...] = jnp.zeros(recon_ref.shape, F32)
            if k < N:
                loop(0, W, own_term(k))
            else:
                loop(0, H, far_term)
            p_out[k] = recon_ref[...].astype(BF)
            share(k).start()

    recon_ref[...] = jnp.zeros(recon_ref.shape, F32)
    loop(0, W, own_term(0))

    def inside_term(k, j):
        if k < N:
            recon_ref[...] += dot(acts[k, j], near[k, col(j), :])
        else:
            recon_ref[...] += dot(acts[k, j], far[col(j - H), :])

    def act_forwards(k, j, act):
        if k % 2 == 0 and k < N:
            @pl.when(even)
            def _():
                act(act_pass(k, k + 1, j, b + 1))

            @pl.when(odd)
            def _():
                act(act_pass(k, k - 1, j, b - 1))
        if k == N - 1:
            @pl.when(j >= H)
            def _():
                act(act_pass(k, N, j, b + 1))

    def arrival(k, j):
        return remote(acts.at[k, j], acts.at[k, j], ad_s.at[k, j], a_r.at[k, j], b, w)

    def inner(d):
        j = blk(d)
        for k in list(range(2, N, 2)) + [N - 1, N]:
            cond = b >= k
            if k >= N - 1:
                cond = cond & even
            if k == N:
                cond = cond & (j >= H)

            @pl.when(cond)
            def _():
                arrival(k, j).wait_recv()
                act_forwards(k, j, start)
                inside_term(k, j)

    loop(0, W, inner)

    def passed(d):
        j = blk(d)
        for k in list(range(1, N, 2)) + [N]:
            cond = b >= k
            if k >= N - 1:
                cond = cond & odd
            if k == N:
                cond = cond & (j >= H)

            @pl.when(cond)
            def _():
                arrival(k, j).wait_recv()
                inside_term(k, j)

    loop(0, W, passed)
    for k in range(1, N + 1):
        @pl.when(b + k >= B)
        def _():
            remote(p_out.at[k], p_in.at[k], p_s.at[k], p_r.at[k], b, w).wait_recv()
            recon_ref[...] += p_in[k].astype(F32)

    og[0] = (recon_ref[...] - tgt_ref[...].astype(F32)).astype(BF)
    for k in range(1, N + 1):
        @pl.when(b + k >= B)
        def _():
            out_grad(k).start()

    def back(d):
        j = blk(d)
        for k in list(range(1, N, 2)) + [N] + list(range(2, N, 2)):
            cond = b >= k
            if k == N:
                cond = cond & (j >= H)

            @pl.when(cond)
            def _():
                rows = near[k, col(j), :] if k < N else far[col(j - H), :]
                terms[k, j] = dot_t(og[0], rows).astype(BF)
                duo_sends(k, j, start)

    def duo_sends(k, j, act):
        if k % 2 == 1 and k <= N - 3:
            @pl.when(even)
            def _():
                act(duo_copy(k, k + 1, j, b + 1))
        if k == 1:
            @pl.when(odd)
            def _():
                act(ret_copy(1, j, b - 1))
        if k % 2 == 1 and k >= 3:
            @pl.when(odd)
            def _():
                act(duo_copy(k, k - 1, j, b - 1))
        if k == N:
            @pl.when(odd)
            def _():
                act(duo_copy(N, N - 1, j, b - 1))

            @pl.when(even)
            def _():
                act(ret_copy(N, j, b - N))

    loop(1, W + 1, back)

    def duo_add(k, j):
        remote(duo.at[k, j], duo.at[k, j], d_s.at[k, j], d_r.at[k, j], b, w).wait_recv()
        terms[k, j] = (terms[k, j].astype(F32) + duo[k, j].astype(F32)).astype(BF)

    def down(d):
        j = blk(d)
        for k in range(2, N, 2):
            @pl.when(b >= k)
            def _():
                duo_add(k, j)
                ret_copy(k, j, b - k).start()

        @pl.when(even & (b >= N - 1))
        def _():
            @pl.when(j >= H)
            def _():
                duo_add(N - 1, j)
            ret_copy(N - 1, j, b - (N - 1)).start()

    loop(1, W + 1, down)

    for k in range(1, N + 1):
        @pl.when(b < k)
        def _():
            remote(og.at[k], og.at[k], o_s.at[k], o_r.at[k], b, w).wait_recv()

    def own_back(j):
        own[j] = dot_t(og[0], near[0, col(j), :])
        for k in range(1, N):
            @pl.when(b < k)
            def _():
                own[j] += dot_t(og[k], near[k, col(j), :])

        @pl.when((b < N) & (j < H))
        def _():
            own[j] += dot_t(og[N], far[col(j), :])

    loop(0, W, own_back)

    def ret_add(k, j):
        remote(ret.at[k, j], ret.at[k, j], r_s.at[k, j], r_r.at[k, j], b, w).wait_recv()
        own[j] += ret[k, j].astype(F32)

    def collect(j):
        @pl.when(even)
        def _():
            ret_add(1, j)
        for k in range(2, N, 2):
            @pl.when(b + k < B)
            def _():
                ret_add(k, j)

        @pl.when(odd & (b + N - 1 < B))
        def _():
            ret_add(N - 1, j)

        @pl.when(even & (b + N < B) & (j >= H))
        def _():
            ret_add(N, j)

    def third(d):
        j = blk(d)
        collect(j)
        z3_out[j] = own[j].astype(BF)
        z3(j).start()

    loop(1, W, third)
    collect(w)

    def gather3(d):
        j = blk(d)
        z3_arrival(j).wait_recv()
        own[w] += z3_in[j].astype(F32)

    loop(1, W, gather3)
    pg[w] = (mask() * own[w]).astype(BF)
    loop(1, W, lambda d: z4(blk(d)).start())
    pg_ref[:, col(w)] = pg[w]

    def gather4(d):
        j = blk(d)
        z4_arrival(j).wait_recv()
        pg_ref[:, col(j)] = pg[j]

    loop(1, W, gather4)

    def drain(d):
        j = blk(d)
        z1(j).wait_send()
        z2(j).wait_send()
        z3(j).wait_send()
        z4(j).wait_send()

    loop(1, W, drain)

    def drain_blk(j):
        act_sends(j, end)
        for k in list(range(2, N, 2)) + [N - 1]:
            cond = b >= k
            if k == N - 1:
                cond = cond & even

            @pl.when(cond)
            def _():
                act_forwards(k, j, end)
        for k in range(1, N + 1):
            cond = b >= k
            if k == N:
                cond = cond & (j >= H)

            @pl.when(cond)
            def _():
                duo_sends(k, j, end)
        for k in range(2, N, 2):
            @pl.when(b >= k)
            def _():
                ret_copy(k, j, b - k).wait_send()

        @pl.when(even & (b >= N - 1))
        def _():
            ret_copy(N - 1, j, b - (N - 1)).wait_send()

    loop(0, W, drain_blk)
    for k in range(1, N + 1):
        @pl.when(b < k)
        def _():
            share(k).wait_send()

        @pl.when(b + k >= B)
        def _():
            out_grad(k).wait_send()


def weight_kernel(x_ref, pg_ref, grad_ref, bias_ref):
    grads = pg_ref[...]
    grad_ref[...] = lax.dot_general(
        x_ref[...], grads, (((0,), (0,)), ((), ())), preferred_element_type=F32
    ).astype(BF)
    bias_ref[...] = jnp.sum(grads.astype(F32), axis=0, keepdims=True)


def on_device(B, W, inputs, encoder, enc_bias, active_blocks, near_decoders, far_decoders, targets):
    N = B // 2
    x = inputs[0]
    tok, width = x.shape
    feats = encoder.shape[2]
    half = far_decoders.shape[1]
    out_cols = targets.shape[2]
    C = feats // W
    dma = pltpu.SemaphoreType.DMA
    blocks = lambda *lead: pltpu.VMEM((*lead, tok, C), BF)
    rows = lambda *lead: pltpu.VMEM((*lead, tok, out_cols), BF)
    vmem = pl.BlockSpec(memory_space=pltpu.VMEM)
    hbm = pl.BlockSpec(memory_space=pl.ANY)
    recon, pre_grad = pl.pallas_call(
        functools.partial(step_kernel, B, W, C, feats // active_blocks.shape[2]),
        out_shape=(jax.ShapeDtypeStruct((tok, out_cols), F32), jax.ShapeDtypeStruct((tok, feats), BF)),
        in_specs=[vmem, hbm, vmem, vmem, hbm, hbm, vmem],
        out_specs=(vmem, vmem),
        scratch_shapes=[
            pltpu.VMEM((width, feats), BF),
            pltpu.VMEM((N, feats, out_cols), BF),
            pltpu.VMEM((half, out_cols), BF),
            blocks(W), blocks(W), blocks(N + 1, W),
            rows(N + 1), rows(N + 1), rows(N + 1),
            blocks(N + 1, W), blocks(N, W), blocks(N + 1, W),
            pltpu.VMEM((W, tok, C), F32),
            blocks(W), blocks(W), blocks(W),
            dma((W,)), dma((N,)), dma,
            dma((W,)), dma((W,)), dma((W,)), dma((W,)),
            dma((N + 1, W)), dma((N + 1, W)), dma((N + 1, W)),
            dma((N + 1,)), dma((N + 1,)), dma((N + 1,)), dma((N + 1,)),
            dma((N + 1, W)), dma((N, W)), dma((N + 1, W)), dma((N + 1, W)),
            dma((W,)), dma((W,)), dma((W,)), dma((W,)),
        ],
        compiler_params=pltpu.CompilerParams(
            collective_id=0, has_side_effects=True, vmem_limit_bytes=67_000_000),
        name="step",
    )(x, encoder[0], enc_bias, active_blocks[0], near_decoders[0], far_decoders[0], targets[0])
    tile = min(feats, 1024)
    enc_grad, bias_grad = pl.pallas_call(
        weight_kernel,
        grid=(feats // tile,),
        out_shape=(jax.ShapeDtypeStruct((width, feats), BF), jax.ShapeDtypeStruct((1, feats), F32)),
        in_specs=[pl.BlockSpec((tok, width), lambda i: (0, 0)), pl.BlockSpec((tok, tile), lambda i: (0, i))],
        out_specs=(pl.BlockSpec((width, tile), lambda i: (0, i)), pl.BlockSpec((1, tile), lambda i: (0, i))),
        name="weights",
    )(x, pre_grad)
    return recon[None], enc_grad[None], bias_grad


def solution(mesh):
    return jax.shard_map(
        functools.partial(on_device, mesh.shape["blk"], mesh.shape["width"]),
        mesh=mesh,
        in_specs=(
            P("blk", None, "width"),
            P("blk", "width", None),
            P("blk", None),
            P("blk", None, None),
            P("blk", None, None, "width"),
            P("blk", None, "width"),
            P("blk", None, "width"),
        ),
        out_specs=(P("blk", None, "width"), P("blk", "width", None), P("blk", None)),
        check_vma=False,
    )
```

time: 475 us -> 168 us (0.35)
  waiting for transfers between devices: 374 us -> 0 us
  Pallas kernels: 0 us -> 164 us
  matrix products: 44.4 us -> 0 us
  starting transfers between devices: 16.7 us -> 0 us
  between operations: 14.3 us -> 0.64 us
  local copies, waits for them, and re-layouts: 14.1 us -> 3.12 us
  other arithmetic: 7.88 us -> 0 us
    reduce_scatter x3 -> x0, waiting for transfers between devices: 183 us -> none  [the longest x1 88.8 us: on_device(): lax.psum_scatter(own_grad, 'width', scatter_dimension=1, tiled=True)]
    pallas_call x0 -> x2, Pallas kernels: none -> 164 us  [the longest x1 159 us: on_device(): pl.pallas_call(functools.partial(step_kernel, B, W, C, feats // active_bl...]
    ppermute x8 -> x0, waiting for transfers between devices: 112 us -> none  [shifted(): return lax.ppermute(block, axis, route)]
    all_gather x3 -> x0, waiting for transfers between devices: 79 us -> none  [the longest x1 27.5 us: on_device(): lax.all_gather((mask_slice * grad_part).astype(jnp.bfloat16), 'width', ax...]
    dot_general x12 -> x0, matrix products: 44.4 us -> none  [the longest x5 18.3 us: forward_product(): return jnp.dot(activations, weights, preferred_element_type=jnp.float32)]
    ppermute x8 -> x0, starting transfers between devices: 16.5 us -> none  [shifted(): return lax.ppermute(block, axis, route)]
    unnamed x20 -> x2, local copies, waits for them, and re-layouts: 10 us -> 3.12 us
    convert_element_type x4 -> x0, other arithmetic: 5.58 us -> none  [the longest x1 1.98 us: on_device(): act_part = (mask_part * (shard_pre + bias_part)).astype(jnp.bfloat16)]
  transfers between devices with their start and end apart: 14 -> 0, of which waited for: 12 -> 0; matrix products, arithmetic and copies ran while one was open for 7% -> 0% of each run, Pallas kernels for 0% -> 0%
where the time goes in v1:
time: 168 us; the launch traced here: 167 us
  Pallas kernels  164 us (98%)
  local copies, waits for them, and re-layouts  3.12 us (2%)
    pallas_call x1, Pallas kernels, on_device(): pl.pallas_call(functools.partial(step_kernel, B, W, C, feats // active_bl...  159 us
    pallas_call x1, Pallas kernels, on_device(): pl.pallas_call(weight_kernel, grid=(feats // tile,), out_shape=(jax.Shape...  4.83 us

profile of v1, /device:TPU:16, one launch (start us, length us, event | category | flops | bytes accessed | tf_op | source)
XLA Modules:
  0.0 167.5 jit_solution(12728832414251800)
XLA Ops:
  0.6 1.4 copy.10
  2.1 158.9 %step.1 = (f32[128,512]{1,0:T(8,128)}, bf16[128,4096]{1,0:T(8,128)(2,1)}) custom-call(bf16[128,512]{1,0:T(8,128)(2,1)} %bitcast.11, bf16[512,4096]{1,0:T(8,128)(2,1)} %bitcast.9, f32[1,4096]{1,0:T(1,128)} %bias_ref.1, s32[128,32]{1,0:T(8,128)} %bitcast.13, bf16[4,4096,512]{2,1,0:T(8,128)(2,1)} %bitcast.8, bf16[2048,512]{1,0:T(8,128)(2,1)} %bitcast.10, ...), custom_call_target="tpu_custom_call" | custom-call | tf_op jit(solution)/shard_map/step/pallas_call | solution.py:450
  161.0 4.8 %weights.1 = (bf16[512,4096]{1,0:T(8,128)(2,1)}, f32[1,4096]{1,0:T(1,128)}) custom-call(bf16[128,512]{1,0:T(8,128)(2,1)} %bitcast.12, bf16[128,4096]{1,0:T(8,128)(2,1)} %get-tuple-element.8.pg_ref), custom_call_target="tpu_custom_call" | custom-call | tf_op jit(solution)/shard_map/weights/pallas_call | solution.py:476
  165.8 1.7 copy.12

commit v2 on v1

--- a/solution.py
+++ b/solution.py
@@ -30,6 +30,11 @@
     w = lax.axis_index("width")
     even = lax.rem(b, 2) == 0
     odd = lax.rem(b, 2) == 1
+    relay = N == 4
+    mid = (b >= N - 2) & (b < N) & relay
+    top = (b >= B - 2) & relay
+    not_mid = jnp.logical_not(mid)
+    not_top = jnp.logical_not(top)
 
     def col(j):
         return pl.ds(pl.multiple_of(j * C, C), C)
@@ -137,7 +142,7 @@
 
     def act_sends(j, act):
         for k in range(2, N, 2):
-            @pl.when(b + k < B)
+            @pl.when((b + k < B) & not_mid)
             def _():
                 act(act_direct(k, j))
 
@@ -145,11 +150,11 @@
         def _():
             act(act_pass(0, 1, j, b + 1))
 
-        @pl.when(odd & (b + N - 1 < B))
+        @pl.when(odd & (b + N - 1 < B) & not_mid)
         def _():
             act(act_direct(N - 1, j))
 
-        @pl.when(even & (b + N < B) & (j >= H))
+        @pl.when(mid | (even & (b + N < B) & (j >= H)))
         def _():
             act(act_direct(N, j))
 
@@ -212,12 +217,28 @@
     def arrival(k, j):
         return remote(acts.at[k, j], acts.at[k, j], ad_s.at[k, j], a_r.at[k, j], b, w)
 
+    def relay_sends(j, act):
+        act(act_pass(N, 2, j, b - 2))
+
+        @pl.when(odd)
+        def _():
+            act(act_pass(N, N - 1, j, b - 1))
+
     def inner(d):
         j = blk(d)
+        if relay:
+            @pl.when(top)
+            def _():
+                arrival(N, j).wait_recv()
+                relay_sends(j, start)
+
+                @pl.when(j >= H)
+                def _():
+                    inside_term(N, j)
         for k in list(range(2, N, 2)) + [N - 1, N]:
             cond = b >= k
             if k >= N - 1:
-                cond = cond & even
+                cond = cond & even & not_top
             if k == N:
                 cond = cond & (j >= H)
 
@@ -233,8 +254,10 @@
         j = blk(d)
         for k in list(range(1, N, 2)) + [N]:
             cond = b >= k
-            if k >= N - 1:
-                cond = cond & odd
+            if k == N - 1:
+                cond = cond & (odd | top)
+            if k == N:
+                cond = cond & odd & not_top
             if k == N:
                 cond = cond & (j >= H)
 
@@ -393,11 +416,15 @@
         for k in list(range(2, N, 2)) + [N - 1]:
             cond = b >= k
             if k == N - 1:
-                cond = cond & even
+                cond = cond & even & not_top
 
             @pl.when(cond)
             def _():
                 act_forwards(k, j, end)
+        if relay:
+            @pl.when(top)
+            def _():
+                relay_sends(j, end)
         for k in range(1, N + 1):
             cond = b >= k
             if k == N:

time: 168 us -> 165 us (0.982)
  Pallas kernels: 164 us -> 161 us
    pallas_call x1, Pallas kernels: 159 us -> 156 us  [on_device(): pl.pallas_call(functools.partial(step_kernel, B, W, C, feats // active_bl...]
where the time goes in v2:
time: 165 us
  Pallas kernels  161 us (98%)
  local copies, waits for them, and re-layouts  3.12 us (2%)
    pallas_call x1, Pallas kernels, on_device(): pl.pallas_call(functools.partial(step_kernel, B, W, C, feats // active_bl...  156 us
    pallas_call x1, Pallas kernels, on_device(): pl.pallas_call(weight_kernel, grid=(feats // tile,), out_shape=(jax.Shape...  4.83 us

profile of v2, /device:TPU:16, one launch (start us, length us, event | category | flops | bytes accessed | tf_op | source)
XLA Modules:
  0.0 164.8 jit_solution(10106720882214918251)
XLA Ops:
  0.6 1.4 copy.10
  2.1 156.2 %step.1 = (f32[128,512]{1,0:T(8,128)}, bf16[128,4096]{1,0:T(8,128)(2,1)}) custom-call(bf16[128,512]{1,0:T(8,128)(2,1)} %bitcast.11, bf16[512,4096]{1,0:T(8,128)(2,1)} %bitcast.9, f32[1,4096]{1,0:T(1,128)} %bias_ref.1, s32[128,32]{1,0:T(8,128)} %bitcast.13, bf16[4,4096,512]{2,1,0:T(8,128)(2,1)} %bitcast.8, bf16[2048,512]{1,0:T(8,128)(2,1)} %bitcast.10, ...), custom_call_target="tpu_custom_call" | custom-call | tf_op jit(solution)/shard_map/step/pallas_call | solution.py:477
  158.3 4.8 %weights.1 = (bf16[512,4096]{1,0:T(8,128)(2,1)}, f32[1,4096]{1,0:T(1,128)}) custom-call(bf16[128,512]{1,0:T(8,128)(2,1)} %bitcast.12, bf16[128,4096]{1,0:T(8,128)(2,1)} %get-tuple-element.8.pg_ref), custom_call_target="tpu_custom_call" | custom-call | tf_op jit(solution)/shard_map/weights/pallas_call | solution.py:503
  163.1 1.7 %copy.12 = f32[1,128,512]{2,1,0:T(8,128)} copy(f32[1,128,512]{2,1,0:T(8,128)} %bitcast.14) | data formatting | bytes 524288
